TPU v7x, 32 devices: a whole 2x2x4 slice. The times are simulated.
32 devices in a mesh: node: 16 (over z, x, core), head: 2 (over y).
Axes of the slice: x: 2, y: 2, z: 4, core: 2. Of those that a mesh axis runs over, the one named last changes fastest.
Arguments:
- features: bfloat16 [32768, 100], P('node'), may hold values from -6 to 6
- proj_weight: bfloat16 [100, 512], P(None, 'head'), may hold values from -0.625 to 0.625
- score_src: float32 [8, 64], P('head'), may hold values from -150 to 150
- score_dst: float32 [8, 64], P('head'), may hold values from -0.75 to 0.75
- request_rows: int32 [16, 16, 512], P('node'), may hold values from 0 to 2047
- slot_index: int32 [8192, 16], P('node'), may hold values from 0 to 8191
- slot_count: int32 [8192], P('node'), may hold values from 1 to 16
- out_weight: bfloat16 [512, 512], replicated, may hold values from -0.25 to 0.25
Outputs:
- layer_out: bfloat16 [8192, 512], P(('node', 'head'))
All inputs are finite; a program needn't handle non-finite values.
Results may differ from a plain program's by a relative error of at most 0.012.
The roundings to bfloat16 on the way count: a program that leaves them out, or rounds other values in their place, can miss the bound.
Values may be sent and summed in bfloat16 or wider, within the bound.
A program may use at most 64 MiB of HBM per device.

v0:
```python
import math

import jax
import jax.numpy as jnp
from jax import lax
from jax.sharding import PartitionSpec as P


def pick_rows(table, row_index):
    total = row_index.shape[0]
    block_rows = math.gcd(total, 1024)
    columns = lax.iota(jnp.int32, table.shape[0])

    def select_block(row_ids):
        hot_table = (row_ids[:, None] == columns[None, :]).astype(table.dtype)
        return jnp.dot(hot_table, table, preferred_element_type=jnp.float32).astype(table.dtype)

    chosen = lax.map(select_block, row_index.reshape(total // block_rows, block_rows))
    return chosen.reshape(total, table.shape[1])


def local(
    features, proj_weight, score_src, score_dst, request_rows, slot_index, slot_count, out_weight
):
    groups = lax.axis_size("node")
    capacity = request_rows.shape[2]
    width = proj_weight.shape[1]
    local_heads = score_src.shape[0]
    head_dim = score_src.shape[1]
    dst_rows = slot_index.shape[0]
    slot_total = slot_index.shape[1]
    wanted = lax.all_to_all(request_rows, "node", split_axis=1, concat_axis=0, tiled=True).reshape(
        groups * capacity
    )
    picked = pick_rows(features, wanted)
    fetched = jnp.einsum(
        "ocf,fw->ocw",
        lax.all_to_all(
            picked.reshape(groups, capacity, features.shape[1]),
            "node",
            split_axis=0,
            concat_axis=0,
            tiled=True,
        ),
        proj_weight,
        preferred_element_type=jnp.float32,
    ).astype(jnp.bfloat16)
    buffer_rows = fetched.reshape(groups * capacity, width)
    zvals = pick_rows(buffer_rows, slot_index.reshape(-1)).reshape(
        dst_rows, slot_total, local_heads, head_dim
    )
    src_part = jnp.einsum("rshd,hd->rsh", zvals.astype(jnp.float32), score_src)
    dst_part = jnp.einsum("rhd,hd->rh", zvals[:, 0].astype(jnp.float32), score_dst)
    logit = src_part + dst_part[:, None, :]
    logit = jnp.where(logit > 0, logit, 0.2 * logit)
    live_mask = (jnp.arange(slot_total, dtype=jnp.int32)[None, :] < slot_count[:, None])[:, :, None]
    logit = jnp.where(live_mask, logit, -1e30)
    peak = jnp.max(logit, axis=1, keepdims=True)
    weights = jnp.where(live_mask, jnp.exp(logit - peak), 0.0)
    alpha = (weights / jnp.sum(weights, axis=1, keepdims=True)).astype(jnp.bfloat16)
    summed = jnp.einsum("rsh,rshd->rhd", alpha, zvals, preferred_element_type=jnp.float32)
    hidden = jax.nn.elu(summed).astype(jnp.bfloat16).reshape(dst_rows, local_heads * head_dim)
    gathered = lax.all_to_all(hidden, "head", split_axis=0, concat_axis=1, tiled=True)
    layer_out = jnp.dot(gathered, out_weight, preferred_element_type=jnp.float32).astype(
        jnp.bfloat16
    )
    return layer_out


def solution(mesh):
    in_specs = (
        P("node", None),
        P(None, "head"),
        P("head", None),
        P("head", None),
        P("node", None, None),
        P("node", None),
        P("node"),
        P(),
    )
    out_specs = P(("node", "head"), None)
    return jax.shard_map(local, mesh=mesh, in_specs=in_specs, out_specs=out_specs, check_vma=False)
```

profile of v0, /device:TPU:0, one launch (start us, length us, event | category | flops | bytes accessed | tf_op | source)
XLA Modules:
  0.0 216.5 jit_solution(17410106399301376929)
XLA Ops:
  1.5 7.4 %all-to-all-start = ((s32[1,16,512]{2,0,1:T(1,128)}), s32[1,16,512]{2,0,1:T(1,128)S(1)}, u32[]{:S(2)}, u32[]{:S(2)}) async-start(s32[1,16,512]{2,0,1:T(1,128)} %copy.25), calls=%async_computation | async-start | bytes 65536 | tf_op jit(solution)/shard_map/all_to_all | solution.py:32
  8.9 6.6 %all-to-all-done = s32[1,16,512]{2,0,1:T(1,128)S(1)} async-done(((s32[1,16,512]{2,0,1:T(1,128)}), s32[1,16,512]{2,0,1:T(1,128)S(1)}, u32[]{:S(2)}, u32[]{:S(2)}) %all-to-all-start) | async-done | bytes 32800 | tf_op jit(solution)/shard_map/all_to_all | solution.py:32
  15.6 28.4 %while.22 = (s32[]{:T(128)}, bf16[8,1024,100]{1,2,0:T(8,128)(2,1)}, s32[8,1024]{1,0:T(8,128)S(1)}, bf16[2048,100]{0,1:T(8,128)(2,1)}, s32[]{:T(128)}) while((s32[]{:T(128)}, bf16[8,1024,100]{1,2,0:T(8,128)(2,1)}, s32[8,1024]{1,0:T(8,128)S(1)}, bf16[2048,100]{0,1:T(8,128)(2,1)}, s32[]{:T(128)}) %tuple.37), condition=%wide.region_1.2_spmd.clone, body=%wide.region_0.1_spmd.clone.sunk | while | flops 421629952 | bytes 651341 | solution.py:18
  19.2 3.5 %fusion.59 = bf16[8,1024,100]{1,2,0:T(8,128)(2,1)} fusion(bf16[8,1024,100]{1,2,0:T(8,128)(2,1)} %get-tuple-element.153, s32[]{:T(128)S(6)} %copy.58, bf16[2048,100]{0,1:T(8,128)(2,1)} %get-tuple-element.160, s32[1024]{0:T(1024)S(1)} %bitcast.68), kind=kOutput, calls=%fused_computation.7.clone.1 | convolution fusion | flops 421629952 | bytes 643076 | tf_op jit(solution)/shard_map/while/body/eval_jaxpr/dot_general | solution.py:16
  22.7 3.5 %fusion.59 = bf16[8,1024,100]{1,2,0:T(8,128)(2,1)} fusion(bf16[8,1024,100]{1,2,0:T(8,128)(2,1)} %get-tuple-element.153, s32[]{:T(128)S(6)} %copy.58, bf16[2048,100]{0,1:T(8,128)(2,1)} %get-tuple-element.160, s32[1024]{0:T(1024)S(1)} %bitcast.68), kind=kOutput, calls=%fused_computation.7.clone.1 | convolution fusion | flops 421629952 | bytes 643076 | tf_op jit(solution)/shard_map/while/body/eval_jaxpr/dot_general | solution.py:16
  29.8 3.5 %fusion.59 = bf16[8,1024,100]{1,2,0:T(8,128)(2,1)} fusion(bf16[8,1024,100]{1,2,0:T(8,128)(2,1)} %get-tuple-element.153, s32[]{:T(128)S(6)} %copy.58, bf16[2048,100]{0,1:T(8,128)(2,1)} %get-tuple-element.160, s32[1024]{0:T(1024)S(1)} %bitcast.68), kind=kOutput, calls=%fused_computation.7.clone.1 | convolution fusion | flops 421629952 | bytes 643076 | tf_op jit(solution)/shard_map/while/body/eval_jaxpr/dot_general | solution.py:16
  33.4 3.5 %fusion.59 = bf16[8,1024,100]{1,2,0:T(8,128)(2,1)} fusion(bf16[8,1024,100]{1,2,0:T(8,128)(2,1)} %get-tuple-element.153, s32[]{:T(128)S(6)} %copy.58, bf16[2048,100]{0,1:T(8,128)(2,1)} %get-tuple-element.160, s32[1024]{0:T(1024)S(1)} %bitcast.68), kind=kOutput, calls=%fused_computation.7.clone.1 | convolution fusion | flops 421629952 | bytes 643076 | tf_op jit(solution)/shard_map/while/body/eval_jaxpr/dot_general | solution.py:16
  36.9 3.6 %fusion.59 = bf16[8,1024,100]{1,2,0:T(8,128)(2,1)} fusion(bf16[8,1024,100]{1,2,0:T(8,128)(2,1)} %get-tuple-element.153, s32[]{:T(128)S(6)} %copy.58, bf16[2048,100]{0,1:T(8,128)(2,1)} %get-tuple-element.160, s32[1024]{0:T(1024)S(1)} %bitcast.68), kind=kOutput, calls=%fused_computation.7.clone.1 | convolution fusion | flops 421629952 | bytes 643076 | tf_op jit(solution)/shard_map/while/body/eval_jaxpr/dot_general | solution.py:16
  47.9 3.5 %copy.27 = bf16[16,512,100]{1,2,0:T(8,128)(2,1)} copy(bf16[16,512,100]{1,0,2:T(8,128)(2,1)} %reshape_reshape.14) | data formatting | bytes 3276800 | tf_op jit(solution)/shard_map/reshape;reshape | solution.py:39
  51.4 3.9 %all-to-all-start.1 = ((bf16[16,512,100]{1,2,0:T(8,128)(2,1)}), bf16[16,512,100]{1,2,0:T(8,128)(2,1)S(1)}, u32[]{:S(2)}, u32[]{:S(2)}) async-start(bf16[16,512,100]{1,2,0:T(8,128)(2,1)} %copy.27), calls=%async_computation.1 | async-start | bytes 3407872 | tf_op jit(solution)/shard_map/all_to_all | solution.py:38
  55.6 33.6 %all-to-all-done.1 = bf16[16,512,100]{1,2,0:T(8,128)(2,1)S(1)} async-done(((bf16[16,512,100]{1,2,0:T(8,128)(2,1)}), bf16[16,512,100]{1,2,0:T(8,128)(2,1)S(1)}, u32[]{:S(2)}, u32[]{:S(2)}) %all-to-all-start.1) | async-done | bytes 1638432 | tf_op jit(solution)/shard_map/all_to_all | solution.py:38
  92.5 67.8 %while.23 = (s32[]{:T(128)}, bf16[8,1024,256]{2,1,0:T(8,128)(2,1)}, s32[8,1024]{1,0:T(8,128)S(1)}, bf16[8192,256]{1,0:T(8,128)(2,1)}, s32[]{:T(128)}) while((s32[]{:T(128)}, bf16[8,1024,256]{2,1,0:T(8,128)(2,1)}, s32[8,1024]{1,0:T(8,128)S(1)}, bf16[8192,256]{1,0:T(8,128)(2,1)}, s32[]{:T(128)}) %tuple.43), condition=%wide.region_3.4_spmd.clone, body=%wide.region_2.3_spmd.clone.sunk | while | flops 4303618048 | bytes 4730957 | solution.py:18
  92.5 8.5 %fusion.61 = bf16[8,1024,256]{2,1,0:T(8,128)(2,1)} fusion(bf16[8,1024,256]{2,1,0:T(8,128)(2,1)} %get-tuple-element.168, s32[]{:T(128)S(6)} %copy.64, bf16[8192,256]{1,0:T(8,128)(2,1)} %get-tuple-element.175, s32[1024]{0:T(1024)S(1)} %bitcast.69), kind=kOutput, calls=%fused_computation.14.clone.1 | convolution fusion | flops 4303618048 | bytes 4722692 | tf_op jit(solution)/shard_map/while/body/eval_jaxpr/dot_general | solution.py:16
  101.0 8.5 %fusion.61 = bf16[8,1024,256]{2,1,0:T(8,128)(2,1)} fusion(bf16[8,1024,256]{2,1,0:T(8,128)(2,1)} %get-tuple-element.168, s32[]{:T(128)S(6)} %copy.64, bf16[8192,256]{1,0:T(8,128)(2,1)} %get-tuple-element.175, s32[1024]{0:T(1024)S(1)} %bitcast.69), kind=kOutput, calls=%fused_computation.14.clone.1 | convolution fusion | flops 4303618048 | bytes 4722692 | tf_op jit(solution)/shard_map/while/body/eval_jaxpr/dot_general | solution.py:16
  109.6 8.4 %fusion.61 = bf16[8,1024,256]{2,1,0:T(8,128)(2,1)} fusion(bf16[8,1024,256]{2,1,0:T(8,128)(2,1)} %get-tuple-element.168, s32[]{:T(128)S(6)} %copy.64, bf16[8192,256]{1,0:T(8,128)(2,1)} %get-tuple-element.175, s32[1024]{0:T(1024)S(1)} %bitcast.69), kind=kOutput, calls=%fused_computation.14.clone.1 | convolution fusion | flops 4303618048 | bytes 4722692 | tf_op jit(solution)/shard_map/while/body/eval_jaxpr/dot_general | solution.py:16
  118.0 8.4 %fusion.61 = bf16[8,1024,256]{2,1,0:T(8,128)(2,1)} fusion(bf16[8,1024,256]{2,1,0:T(8,128)(2,1)} %get-tuple-element.168, s32[]{:T(128)S(6)} %copy.64, bf16[8192,256]{1,0:T(8,128)(2,1)} %get-tuple-element.175, s32[1024]{0:T(1024)S(1)} %bitcast.69), kind=kOutput, calls=%fused_computation.14.clone.1 | convolution fusion | flops 4303618048 | bytes 4722692 | tf_op jit(solution)/shard_map/while/body/eval_jaxpr/dot_general | solution.py:16
  126.5 8.5 %fusion.61 = bf16[8,1024,256]{2,1,0:T(8,128)(2,1)} fusion(bf16[8,1024,256]{2,1,0:T(8,128)(2,1)} %get-tuple-element.168, s32[]{:T(128)S(6)} %copy.64, bf16[8192,256]{1,0:T(8,128)(2,1)} %get-tuple-element.175, s32[1024]{0:T(1024)S(1)} %bitcast.69), kind=kOutput, calls=%fused_computation.14.clone.1 | convolution fusion | flops 4303618048 | bytes 4722692 | tf_op jit(solution)/shard_map/while/body/eval_jaxpr/dot_general | solution.py:16
  135.0 8.5 %fusion.61 = bf16[8,1024,256]{2,1,0:T(8,128)(2,1)} fusion(bf16[8,1024,256]{2,1,0:T(8,128)(2,1)} %get-tuple-element.168, s32[]{:T(128)S(6)} %copy.64, bf16[8192,256]{1,0:T(8,128)(2,1)} %get-tuple-element.175, s32[1024]{0:T(1024)S(1)} %bitcast.69), kind=kOutput, calls=%fused_computation.14.clone.1 | convolution fusion | flops 4303618048 | bytes 4722692 | tf_op jit(solution)/shard_map/while/body/eval_jaxpr/dot_general | solution.py:16
  143.4 8.4 %fusion.61 = bf16[8,1024,256]{2,1,0:T(8,128)(2,1)} fusion(bf16[8,1024,256]{2,1,0:T(8,128)(2,1)} %get-tuple-element.168, s32[]{:T(128)S(6)} %copy.64, bf16[8192,256]{1,0:T(8,128)(2,1)} %get-tuple-element.175, s32[1024]{0:T(1024)S(1)} %bitcast.69), kind=kOutput, calls=%fused_computation.14.clone.1 | convolution fusion | flops 4303618048 | bytes 4722692 | tf_op jit(solution)/shard_map/while/body/eval_jaxpr/dot_general | solution.py:16
  151.9 8.5 %fusion.61 = bf16[8,1024,256]{2,1,0:T(8,128)(2,1)} fusion(bf16[8,1024,256]{2,1,0:T(8,128)(2,1)} %get-tuple-element.168, s32[]{:T(128)S(6)} %copy.64, bf16[8192,256]{1,0:T(8,128)(2,1)} %get-tuple-element.175, s32[1024]{0:T(1024)S(1)} %bitcast.69), kind=kOutput, calls=%fused_computation.14.clone.1 | convolution fusion | flops 4303618048 | bytes 4722692 | tf_op jit(solution)/shard_map/while/body/eval_jaxpr/dot_general | solution.py:16
  160.4 12.9 %reshape_reshape.15 = bf16[512,16,4,64]{3,2,1,0:T(4,128)(2,1)} reshape(bf16[8,1024,256]{2,1,0:T(8,128)(2,1)} %get-tuple-element.60) | data formatting | bytes 8388608 | tf_op jit(solution)/shard_map/reshape;reshape | solution.py:49
  174.7 13.0 %multiply_reduce_fusion.1 = f32[4,512,16]{0,2,1:T(8,128)} fusion(f32[4,64]{1,0:T(4,128)S(1)} %copy-done.4, bf16[512,16,4,64]{3,2,1,0:T(4,128)(2,1)} %reshape_reshape.15), kind=kLoop, calls=%fused_computation.19 | loop fusion | flops 6258688 | bytes 4326400
  194.2 11.7 %multiply_reduce_fusion = f32[512,4,64]{2,1,0:T(4,128)S(1)} fusion(f32[512,4,16]{1,2,0:T(8,128)} %copy.48, bf16[512,16,4,64]{3,2,1,0:T(4,128)(2,1)} %reshape_reshape.15), kind=kLoop, calls=%fused_computation.18 | loop fusion | flops 6160384 | bytes 4849664
  206.5 9.0 %all_to_all.33 = bf16[2,256,256]{1,2,0:T(8,128)(2,1)S(1)} all-to-all(bf16[2,256,256]{1,2,0:T(8,128)(2,1)S(1)} %copy.28), channel_id=1, replica_groups=mesh['node'=16,'head'=2] {'head'}, dimensions={0} | all-to-all | bytes 524288 | tf_op jit(solution)/shard_map/all_to_all | solution.py:63
  (53 shorter events, 29.3 us)
Async XLA Ops:
  0.0 215.5 %copy-start = (bf16[512,512]{1,0:T(8,128)(2,1)S(1)}, bf16[512,512]{1,0:T(8,128)(2,1)}, u32[]{:S(2)}) copy-start(bf16[512,512]{1,0:T(8,128)(2,1)} %param.19) | copy-start | bytes 1572868
  1.5 14.0 %all-to-all-start = ((s32[1,16,512]{2,0,1:T(1,128)}), s32[1,16,512]{2,0,1:T(1,128)S(1)}, u32[]{:S(2)}, u32[]{:S(2)}) async-start(s32[1,16,512]{2,0,1:T(1,128)} %copy.25), calls=%async_computation | async-start | bytes 65536 | tf_op jit(solution)/shard_map/all_to_all | solution.py:32
  47.9 7.5 %copy-start.2 = (s32[512,16]{0,1:T(8,128)S(1)}, s32[512,16]{0,1:T(8,128)}, u32[]{:S(2)}) copy-start(s32[512,16]{0,1:T(8,128)} %param.17) | copy-start | bytes 98308
  47.9 7.8 %copy-start.3 = (s32[512]{0:T(512)S(1)}, s32[512]{0:T(512)}, u32[]{:S(2)}) copy-start(s32[512]{0:T(512)} %param.18) | copy-start | bytes 6148
  47.9 41.3 %copy-start.1 = (bf16[100,256]{1,0:T(8,128)(2,1)S(1)}, bf16[100,256]{1,0:T(8,128)(2,1)}, u32[]{:S(2)}) copy-start(bf16[100,256]{1,0:T(8,128)(2,1)} %param.13) | copy-start | bytes 153604
  51.4 37.8 %all-to-all-start.1 = ((bf16[16,512,100]{1,2,0:T(8,128)(2,1)}), bf16[16,512,100]{1,2,0:T(8,128)(2,1)S(1)}, u32[]{:S(2)}, u32[]{:S(2)}) async-start(bf16[16,512,100]{1,2,0:T(8,128)(2,1)} %copy.27), calls=%async_computation.1 | async-start | bytes 3407872 | tf_op jit(solution)/shard_map/all_to_all | solution.py:38
  160.4 14.1 %copy-start.5 = (f32[4,64]{1,0:T(4,128)S(1)}, f32[4,64]{1,0:T(4,128)}, u32[]{:S(2)}) copy-start(f32[4,64]{1,0:T(4,128)} %param.15) | copy-start | bytes 3076
  160.4 14.4 %copy-start.4 = (f32[4,64]{1,0:T(4,128)S(1)}, f32[4,64]{1,0:T(4,128)}, u32[]{:S(2)}) copy-start(f32[4,64]{1,0:T(4,128)} %param.14) | copy-start | bytes 3076
where the time goes:
time: 221 us; the launch traced here: 217 us
  matrix products  101 us (46%)
  waiting for transfers between devices  40.2 us (18%)
  local copies, waits for them, and re-layouts  30.2 us (14%)
  other arithmetic  25 us (11%)
  starting transfers between devices  11.3 us (5%)
  blocking collectives  8.95 us (4%)
    dot_general x16, matrix products, select_block(): jnp.dot(hot_table, table, preferred_element_type=jnp.float32)  96.1 us
    all_to_all x1, waiting for transfers between devices, local(): lax.all_to_all(picked.reshape(groups, capacity, features.shape[1]), 'node...  33.6 us
    unnamed x2, other arithmetic  24.7 us
    another operation x1, local copies, waits for them, and re-layouts, local(): pick_rows(buffer_rows, slot_index.reshape(-1))  12.9 us
    all_to_all x1, blocking collectives, local(): lax.all_to_all(hidden, 'head', split_axis=0, concat_axis=1, tiled=True)  8.95 us
    all_to_all x1, starting transfers between devices, local(): lax.all_to_all(request_rows, 'node', split_axis=1, concat_axis=0, tiled=T...  7.39 us
    all_to_all x1, waiting for transfers between devices, local(): lax.all_to_all(request_rows, 'node', split_axis=1, concat_axis=0, tiled=T...  6.62 us
    unnamed x15, local copies, waits for them, and re-layouts  5.08 us
  transfers between devices with their start and end apart: 2, of which 2 were waited for; matrix products, arithmetic and copies ran while one was open for 0% of the time, Pallas kernels for 0%

commit v1 on v0

v1 whole, which is shorter than its diff:
```python
import functools

import jax
import jax.numpy as jnp
from jax import lax
from jax.experimental import pallas as pl
from jax.experimental.pallas import tpu as pltpu
from jax.sharding import PartitionSpec as P

LANES = 128


def quotient(value, divisor):
    if divisor & (divisor - 1) == 0:
        return lax.shift_right_logical(value, divisor.bit_length() - 1)
    return lax.div(value, divisor)


def elu(x):
    series = x * (1.0 + x * (0.5 + x * (1 / 6 + x * (1 / 24 + x * (1 / 120)))))
    below = jnp.where(x > -0.1, series, jnp.exp(jnp.minimum(x, 0.0)) - 1.0)
    return jnp.where(x > 0, x, below)


def address_rows(slot_ref, request_ref, where_ref, owned, capacity):
    unroll = 16

    def body(step, carry):
        for k in range(unroll):
            place = step * unroll + k
            b = slot_ref[place]
            where_ref[place] = quotient(b, capacity) * owned + request_ref[b]
        return carry

    lax.fori_loop(0, where_ref.shape[0] // unroll, body, 0)


def gather_rows(where_ref, table_ref, picked_ref):
    unroll = 64

    def body(step, carry):
        base = pl.multiple_of(step * unroll, unroll)
        for k in range(unroll):
            picked_ref[pl.ds(base + k, 1), :] = table_ref[pl.ds(where_ref[base + k], 1), :]
        return carry

    lax.fori_loop(0, picked_ref.shape[0] // unroll, body, 0)


def score_matrix(row, heads, head_dim):
    width = row.shape[1]
    hi = row.astype(jnp.bfloat16).astype(jnp.float32)
    mid = (row - hi).astype(jnp.bfloat16).astype(jnp.float32)
    lo = row - hi - mid
    at = lax.broadcasted_iota(jnp.int32, (LANES, width), 0)
    head_of = quotient(lax.broadcasted_iota(jnp.int32, (LANES, width), 1), head_dim)
    total = jnp.zeros((LANES, width), jnp.float32)
    for place, term in enumerate((hi, mid, lo)):
        total = jnp.where(at == head_of + place * heads, term, total)
    return total.astype(jnp.bfloat16)


def scores(zvals, matrix, heads):
    parts = lax.dot_general(
        zvals, matrix, (((1,), (1,)), ((), ())), preferred_element_type=jnp.float32
    )
    return parts + (
        pltpu.roll(parts, LANES - heads, 1) + pltpu.roll(parts, LANES - 2 * heads, 1)
    )


def attend(heads, weights_ref, count_ref, out_weight_ref, out_ref, picked_ref, z_ref, logit_ref):
    rows, width = out_ref.shape[0], out_weight_ref.shape[0]
    feat = picked_ref.shape[1]
    slots = z_ref.shape[0]
    head_dim = width // heads
    proj = weights_ref[0:feat, :].astype(jnp.bfloat16)
    src = score_matrix(weights_ref[feat : feat + 1, :], heads, head_dim)
    dst = score_matrix(weights_ref[feat + 1 : feat + 2, :], heads, head_dim)
    spread = (
        lax.broadcasted_iota(jnp.int32, (LANES, width), 0)
        == quotient(lax.broadcasted_iota(jnp.int32, (LANES, width), 1), head_dim)
    ).astype(jnp.bfloat16)

    def project(s):
        picked = picked_ref[pl.ds(pl.multiple_of(s * rows, rows), rows), :].astype(jnp.bfloat16)
        z = jnp.dot(picked, proj, preferred_element_type=jnp.float32).astype(jnp.bfloat16)
        z_ref[s] = z
        return z

    z0 = project(0)
    dst_part = scores(z0, dst, heads)
    count = count_ref[...]

    def logits(s, peak):
        z = project(s)
        logit = scores(z, src, heads) + dst_part
        logit = jnp.where(logit > 0, logit, 0.2 * logit)
        logit = jnp.where(s < count, logit, -1e30)
        logit_ref[s] = logit
        return jnp.maximum(peak, logit)

    peak = lax.fori_loop(0, slots, logits, jnp.full((rows, LANES), -1e30, jnp.float32))

    def weigh(s, total):
        weight = jnp.where(s < count, jnp.exp(logit_ref[s] - peak), 0.0)
        logit_ref[s] = weight
        return total + weight

    total = lax.fori_loop(0, slots, weigh, jnp.zeros((rows, LANES), jnp.float32))
    inverse = 1.0 / total

    def combine(s, summed):
        alpha = (logit_ref[s] * inverse).astype(jnp.bfloat16)
        wide = jnp.dot(alpha, spread, preferred_element_type=jnp.float32)
        return summed + wide * z_ref[s].astype(jnp.float32)

    summed = lax.fori_loop(0, slots, combine, jnp.zeros((rows, width), jnp.float32))
    hidden = elu(summed).astype(jnp.bfloat16)
    out_ref[...] = jnp.dot(
        hidden, out_weight_ref[...], preferred_element_type=jnp.float32
    ).astype(jnp.bfloat16)


def kernel(
    owned,
    capacity,
    heads,
    chunks,
    slot_ref,
    request_ref,
    weights_ref,
    count_ref,
    out_weight_ref,
    nodes_ref,
    out_ref,
    where_ref,
    landing_ref,
    table_ref,
    picked_ref,
    z_ref,
    logit_ref,
    sems,
):
    rows = nodes_ref.shape[0] // chunks
    copies = []
    for c in range(chunks):
        part = pl.ds(c * rows, rows)
        copies.append(
            pltpu.make_async_copy(nodes_ref.at[part, :], landing_ref.at[part, :], sems.at[c])
        )
        copies[-1].start()
    address_rows(slot_ref, request_ref, where_ref, owned, capacity)
    for c in range(chunks):
        copies[c].wait()
        block = 256

        def widen(step, carry):
            part = pl.ds(pl.multiple_of(c * rows + step * block, block), block)
            table_ref[part, :] = landing_ref[part, :].astype(jnp.float32)
            return carry

        lax.fori_loop(0, rows // block, widen, 0)
    gather_rows(where_ref, table_ref, picked_ref)
    attend(heads, weights_ref, count_ref, out_weight_ref, out_ref, picked_ref, z_ref, logit_ref)


def local(
    features, proj_weight, score_src, score_dst, request_rows, slot_index, slot_count, out_weight
):
    planes = lax.axis_size("head")
    groups = lax.axis_size("node")
    plane = lax.axis_index("head")
    owned, feat = features.shape
    capacity = request_rows.shape[2]
    heads = score_src.shape[0] * planes
    width = proj_weight.shape[1]
    dst_rows = slot_index.shape[0] // planes
    slots = slot_index.shape[1]

    share = lax.dynamic_slice_in_dim(features, plane * (owned // planes), owned // planes, 0)
    nodes = lax.all_gather(share, ("node", "head"), axis=0, tiled=True)
    mine = jnp.concatenate(
        [
            proj_weight.astype(jnp.float32),
            score_src.reshape(1, width),
            score_dst.reshape(1, width),
        ],
        axis=0,
    )
    weights = lax.all_gather(mine, "head", axis=1, tiled=True)
    slot = lax.dynamic_slice_in_dim(slot_index, plane * dst_rows, dst_rows, 0).T.reshape(-1)
    count = jnp.broadcast_to(
        lax.dynamic_slice_in_dim(slot_count, plane * dst_rows, dst_rows, 0)[:, None],
        (dst_rows, LANES),
    )
    total_nodes = groups * owned
    vmem = pl.BlockSpec(memory_space=pltpu.VMEM)
    smem = pl.BlockSpec(memory_space=pltpu.SMEM)
    chunks = 8
    return pl.pallas_call(
        functools.partial(kernel, owned, capacity, heads, chunks),
        out_shape=jax.ShapeDtypeStruct((dst_rows, out_weight.shape[1]), jnp.bfloat16),
        in_specs=[smem, smem, vmem, vmem, vmem, pl.BlockSpec(memory_space=pl.ANY)],
        out_specs=vmem,
        scratch_shapes=[
            pltpu.SMEM((dst_rows * slots,), jnp.int32),
            pltpu.VMEM((total_nodes, feat), jnp.bfloat16),
            pltpu.VMEM((total_nodes, feat), jnp.float32),
            pltpu.VMEM((dst_rows * slots, feat), jnp.float32),
            pltpu.VMEM((slots, dst_rows, width * planes), jnp.bfloat16),
            pltpu.VMEM((slots, dst_rows, LANES), jnp.float32),
            pltpu.SemaphoreType.DMA((chunks,)),
        ],
        compiler_params=pltpu.CompilerParams(vmem_limit_bytes=67043328),
    )(slot, request_rows.reshape(-1), weights, count, out_weight, nodes)


def solution(mesh):
    in_specs = (
        P("node", None),
        P(None, "head"),
        P("head", None),
        P("head", None),
        P("node", None, None),
        P("node", None),
        P("node"),
        P(),
    )
    out_specs = P(("node", "head"), None)
    return jax.shard_map(local, mesh=mesh, in_specs=in_specs, out_specs=out_specs, check_vma=False)
```

time: 221 us -> 129 us (0.58); the launches traced: 217 us -> 128 us
  matrix products: 101 us -> 0 us
  Pallas kernels: 0 us -> 30.4 us
  waiting for transfers between devices: 40.2 us -> 69.4 us
  other arithmetic: 25 us -> 0.83 us
  local copies, waits for them, and re-layouts: 30.2 us -> 7.52 us
  between operations: 0.15 us -> 13.4 us
  starting transfers between devices: 11.3 us -> 0.01 us
  blocking collectives: 8.95 us -> 6.72 us
    dot_general x19 -> x0, matrix products: 101 us -> none  [the longest x16 96.1 us: select_block(): jnp.dot(hot_table, table, preferred_element_type=jnp.float32)]
    all_gather x0 -> x1, waiting for transfers between devices: none -> 69.4 us  [local(): nodes = lax.all_gather(share, ('node', 'head'), axis=0, tiled=True)]
    all_to_all x2 -> x0, waiting for transfers between devices: 40.2 us -> none  [the longest x1 33.6 us: local(): lax.all_to_all(picked.reshape(groups, capacity, features.shape[1]), 'node...]
    pallas_call x0 -> x1, Pallas kernels: none -> 30.4 us  [local(): pl.pallas_call(functools.partial(kernel, owned, capacity, heads, chunks),...]
    unnamed x2 -> x0, other arithmetic: 24.7 us -> none
    another operation x5 -> x0, local copies, waits for them, and re-layouts: 18.1 us -> none  [the longest x1 12.9 us: local(): pick_rows(buffer_rows, slot_index.reshape(-1))]
    all_to_all x2 -> x0, starting transfers between devices: 11.3 us -> none  [the longest x1 7.39 us: local(): lax.all_to_all(request_rows, 'node', split_axis=1, concat_axis=0, tiled=T...]
    all_to_all x1 -> x0, blocking collectives: 8.95 us -> none  [local(): lax.all_to_all(hidden, 'head', split_axis=0, concat_axis=1, tiled=True)]
  transfers between devices with their start and end apart: 2 -> 1, of which waited for: 2 -> 1; matrix products, arithmetic and copies ran while one was open for 0% -> 5% of each run, Pallas kernels for 0% -> 0%
where the time goes in v1:
time: 129 us; the launch traced here: 128 us
  waiting for transfers between devices  69.4 us (54%)
  Pallas kernels  30.4 us (24%)
  between operations  13.4 us (10%)
  local copies, waits for them, and re-layouts  7.52 us (6%)
  blocking collectives  6.72 us (5%)
    all_gather x1, waiting for transfers between devices, local(): nodes = lax.all_gather(share, ('node', 'head'), axis=0, tiled=True)  69.4 us
    pallas_call x1, Pallas kernels, local(): pl.pallas_call(functools.partial(kernel, owned, capacity, heads, chunks),...  30.4 us
    all_gather x1, blocking collectives, local(): weights = lax.all_gather(mine, 'head', axis=1, tiled=True)  6.72 us
    unnamed x4, local copies, waits for them, and re-layouts  3.55 us
  transfers between devices with their start and end apart: 1, of which 1 were waited for; matrix products, arithmetic and copies ran while one was open for 5% of the time, Pallas kernels for 0%

profile of v1, /device:TPU:0, one launch (start us, length us, event | category | flops | bytes accessed | tf_op | source)
XLA Modules:
  0.0 128.2 jit_solution(12319964479009768545)
XLA Ops:
  6.5 0.0 all-gather.2.cloned.1.call-start
  6.5 0.9 constant_dynamic-slice_fusion
  7.5 0.9 copy.10
  8.3 0.0 all-gather.2.cloned.1.call-update
  8.4 0.8 dynamic_slice.10
  9.1 0.7 dynamic-slice_bitcast_fusion
  9.8 0.6 copy.11
  10.5 0.8 convert_element_type.3
  11.3 0.8 reshape.15
  12.0 0.8 reshape.16
  12.8 1.4 %copy.12 = s32[2,4,8,128]{3,1,2,0:T(4,128)} copy(s32[2,4,8,128]{3,2,1,0:T(8,128)} %bitcast.8) | data formatting | bytes 65536
  14.2 6.7 %all_gather.6.weights_ref = f32[102,512]{1,0:T(8,128)} all-gather(f32[102,256]{1,0:T(8,128)S(1)} %pad_maximum_fusion), channel_id=1, replica_groups=mesh['node'=16,'head'=2] {'head'}, dimensions={1}, use_global_device_ids=true | all-gather | bytes 313344 | tf_op jit(solution)/shard_map/all_gather | solution.py:191
  20.9 69.4 %all-gather.2.cloned.1.call-done.nodes_ref = bf16[32768,100]{1,0:T(8,128)(2,1)} async-done(((bf16[1024,100]{1,0:T(8,128)(2,1)}), bf16[32768,100]{1,0:T(8,128)(2,1)}) %all-gather.2.cloned.1.call-update) | async-done | bytes 6553616 | tf_op jit(solution)/shard_map/all_gather | solution.py:182
  90.3 0.7 broadcast_in_dim.2.count_ref
  91.0 30.4 %shard_map.82 = bf16[256,512]{1,0:T(8,128)(2,1)} custom-call(s32[4096]{0:T(1024)} %bitcast.7, s32[8192]{0:T(1024)} %bitcast.6, f32[102,512]{1,0:T(8,128)} %all_gather.6.weights_ref, s32[256,128]{1,0:T(8,128)} %broadcast_in_dim.2.count_ref, bf16[512,512]{1,0:T(8,128)(2,1)} %out_weight_ref.1, bf16[32768,100]{1,0:T(8,128)(2,1)} %all-gather.2.cloned.1.call-done.nodes_ref), custom_call_target="tpu_custom_call" | custom-call | tf_op jit(solution)/shard_map/pallas_call | solution.py:201
  (1 shorter events, 0.0 us)
Async XLA Ops:
  6.5 83.7 %all-gather.2.cloned.1.call-start = ((), (), s32[]{:S(2)}) async-start(), calls=%async_computation | async-start | bytes 8650752 | tf_op jit(solution)/shard_map/all_gather | solution.py:182
Sparse Core Ops, SparseCore 0:
  10.4 79.8 all-gather.1

commit v2 on v1

v2 whole, which is shorter than its diff:
```python
import functools

import jax
import jax.numpy as jnp
from jax import lax
from jax.experimental import pallas as pl
from jax.experimental.pallas import tpu as pltpu
from jax.sharding import PartitionSpec as P

LANES = 128


def quotient(value, divisor):
    if divisor & (divisor - 1) == 0:
        return lax.shift_right_logical(value, divisor.bit_length() - 1)
    return lax.div(value, divisor)


def elu(x):
    series = x * (1.0 + x * (0.5 + x * (1 / 6 + x * (1 / 24 + x * (1 / 120)))))
    below = jnp.where(x > -0.1, series, jnp.exp(jnp.minimum(x, 0.0)) - 1.0)
    return jnp.where(x > 0, x, below)


def address_rows(first, amount, base, slots, dst_rows, slot_ref, request_ref, where_ref, owned, capacity):
    def body(row, carry):
        for k in range(slots):
            b = slot_ref[base + row, k]
            owner = quotient(b, capacity)
            where_ref[k * dst_rows + row] = owner * owned + request_ref[0, owner, b - owner * capacity]
        return carry

    lax.fori_loop(first, first + amount, body, 0)


def gather_rows(where_ref, table_ref, picked_ref):
    unroll = 64

    def body(step, carry):
        base = pl.multiple_of(step * unroll, unroll)
        for k in range(unroll):
            picked_ref[pl.ds(base + k, 1), :] = table_ref[pl.ds(where_ref[base + k], 1), :]
        return carry

    lax.fori_loop(0, picked_ref.shape[0] // unroll, body, 0)


def score_matrix(score_ref, heads, head_dim):
    table = jnp.concatenate([score_ref[p] for p in range(score_ref.shape[0])], axis=0)
    wide = jnp.concatenate([table] * heads, axis=1)
    shape = (heads, heads * head_dim)
    head_of = quotient(lax.broadcasted_iota(jnp.int32, shape, 1), head_dim)
    row = jnp.where(head_of == lax.broadcasted_iota(jnp.int32, shape, 0), wide, 0.0)
    hi = row.astype(jnp.bfloat16).astype(jnp.float32)
    mid = (row - hi).astype(jnp.bfloat16).astype(jnp.float32)
    lo = row - hi - mid
    rest = jnp.zeros((LANES - 3 * heads, heads * head_dim), jnp.float32)
    return jnp.concatenate([hi, mid, lo, rest], axis=0).astype(jnp.bfloat16)


def scores(zvals, matrix, heads):
    parts = lax.dot_general(
        zvals, matrix, (((1,), (1,)), ((), ())), preferred_element_type=jnp.float32
    )
    return parts + (
        pltpu.roll(parts, LANES - heads, 1) + pltpu.roll(parts, LANES - 2 * heads, 1)
    )


def attend(heads, proj_ref, src_ref, dst_ref, count_ref, out_weight_ref, out_ref, picked_ref, z_ref, logit_ref):
    rows, width = out_ref.shape[0], out_weight_ref.shape[0]
    feat = picked_ref.shape[1]
    slots = z_ref.shape[0]
    head_dim = width // heads
    proj = jnp.concatenate([proj_ref[p] for p in range(proj_ref.shape[0])], axis=1)
    src = score_matrix(src_ref, heads, head_dim)
    dst = score_matrix(dst_ref, heads, head_dim)
    spread = (
        lax.broadcasted_iota(jnp.int32, (LANES, width), 0)
        == quotient(lax.broadcasted_iota(jnp.int32, (LANES, width), 1), head_dim)
    ).astype(jnp.bfloat16)

    def project(s):
        picked = picked_ref[pl.ds(pl.multiple_of(s * rows, rows), rows), :].astype(jnp.bfloat16)
        z = jnp.dot(picked, proj, preferred_element_type=jnp.float32).astype(jnp.bfloat16)
        z_ref[s] = z
        return z

    z0 = project(0)
    dst_part = scores(z0, dst, heads)
    count = count_ref[...]

    def logits(s, peak):
        z = project(s)
        logit = scores(z, src, heads) + dst_part
        logit = jnp.where(logit > 0, logit, 0.2 * logit)
        logit = jnp.where(s < count, logit, -1e30)
        logit_ref[s] = logit
        return jnp.maximum(peak, logit)

    peak = lax.fori_loop(0, slots, logits, jnp.full((rows, LANES), -1e30, jnp.float32))

    def weigh(s, total):
        weight = jnp.where(s < count, jnp.exp(logit_ref[s] - peak), 0.0)
        logit_ref[s] = weight
        return total + weight

    total = lax.fori_loop(0, slots, weigh, jnp.zeros((rows, LANES), jnp.float32))
    inverse = 1.0 / total

    def combine(s, summed):
        alpha = (logit_ref[s] * inverse).astype(jnp.bfloat16)
        wide = jnp.dot(alpha, spread, preferred_element_type=jnp.float32)
        return summed + wide * z_ref[s].astype(jnp.float32)

    summed = lax.fori_loop(0, slots, combine, jnp.zeros((rows, width), jnp.float32))
    hidden = elu(summed).astype(jnp.bfloat16)
    out_ref[...] = jnp.dot(
        hidden, out_weight_ref[...], preferred_element_type=jnp.float32
    ).astype(jnp.bfloat16)


def plan(lines, cores, planes, groups, pieces):
    far = ([1, lines - 1] + list(range(2, lines - 1)))[: lines - 1]
    second, last = [], []
    first = [("z", d, 0, 0, s) for s in range(pieces) for d in far]
    own = [("o", 0, dx, dy, s) for dy in range(planes) for s in range(pieces) for dx in range(1, groups)]
    merged = []
    while first or own:
        merged += first[:2] + own[:1]
        first, own = first[2:], own[1:]
    for s in range(pieces):
        for d in far:
            for dy in range(1, planes):
                second.append(("y", d, 0, dy, s))
        for d in far:
            for dx in range(1, groups):
                second.append(("x", d, dx, 0, s))
    for s in range(pieces):
        for d in far:
            for dx in range(1, groups):
                for dy in range(1, planes):
                    last.append(("d", d, dx, dy, s))
    return far, merged + second + last


def kernel(
    lines,
    groups,
    cores,
    planes,
    pieces,
    capacity,
    heads,
    slot_ref,
    request_ref,
    slot_count_ref,
    proj_in,
    src_in,
    dst_in,
    out_weight_ref,
    nodes_ref,
    out_ref,
    where_ref,
    landing_ref,
    table_ref,
    picked_ref,
    z_ref,
    logit_ref,
    count_ref,
    proj_ref,
    src_ref,
    dst_ref,
    local_sems,
    send_sems,
    recv_sems,
    weight_sems,
):
    owned = nodes_ref.shape[0]
    unit = owned // planes
    piece = unit // pieces
    dst_rows = out_ref.shape[0]
    slots = z_ref.shape[0]
    node, y = lax.axis_index("node"), lax.axis_index("head")
    z = node // (groups * cores)
    x = (node // cores) % groups
    c = node % cores

    def device(dz, dx, dc, dy):
        place = (((z + dz) % lines) * groups + (x + dx) % groups) * cores + (c + dc) % cores
        return {"node": place, "head": (y + dy) % planes}

    def number(dz, dx, dc, dy, s):
        place = (((z + dz) % lines) * groups + (x + dx) % groups) * cores + (c + dc) % cores
        return (place * planes + (y + dy) % planes) * pieces + s

    def part(index):
        return pl.ds(pl.multiple_of(index * piece, piece), piece)

    far, events = plan(lines, cores, planes, groups, pieces)
    peers = [(d, 0, 0, 0) for d in far]
    peers += [(0, d, 0, 0) for d in range(1, groups)]
    peers += [(0, 0, d, 0) for d in range(1, cores)]
    peers += [(0, 0, 0, d) for d in range(1, planes)]
    barrier = pltpu.get_barrier_semaphore()
    for peer in peers:
        pl.semaphore_signal(barrier, inc=1, device_id=device(*peer))
    own_rows = pl.ds(pl.multiple_of(node * owned, owned), owned)
    fetch = [pltpu.make_async_copy(nodes_ref, landing_ref.at[own_rows, :], local_sems.at[0])]
    fetch += [
        pltpu.make_async_copy(given, held.at[y], local_sems.at[1 + i])
        for i, (given, held) in enumerate(((proj_in, proj_ref), (src_in, src_ref), (dst_in, dst_ref)))
    ]
    for copy in fetch:
        copy.start()
    pl.semaphore_wait(barrier, len(peers))
    for copy in fetch:
        copy.wait()

    sent = []

    def send(index, peer):
        view = landing_ref.at[part(index), :]
        copy = pltpu.make_async_remote_copy(
            src_ref=view,
            dst_ref=view,
            send_sem=send_sems.at[len(sent)],
            recv_sem=recv_sems.at[index],
            device_id=device(*peer),
        )
        copy.start()
        sent.append(copy)

    def landed(index):
        view = landing_ref.at[part(index), :]
        pltpu.make_async_remote_copy(
            src_ref=view,
            dst_ref=view,
            send_sem=send_sems.at[0],
            recv_sem=recv_sems.at[index],
            device_id=device(*peers[0]),
        ).wait_recv()

    block = 128 if piece % 128 == 0 else piece

    def widen(index):
        def body(step, carry):
            rows = pl.ds(pl.multiple_of(index * piece + step * block, block), block)
            table_ref[rows, :] = landing_ref[rows, :].astype(jnp.float32)
            return carry

        lax.fori_loop(0, piece // block, body, 0)

    for s in range(pieces):
        for d in far:
            send(number(0, 0, 0, 0, s), (d, 0, 0, 0))
    for dy in range(planes):
        for s in range(pieces):
            for dx in range(1, groups):
                send(number(0, 0, 0, dy, s), (0, dx, 0, 0))
    shared = []
    for i, held in enumerate((proj_ref, src_ref, dst_ref)):
        for dy in range(1, planes):
            copy = pltpu.make_async_remote_copy(
                src_ref=held.at[y],
                dst_ref=held.at[y],
                send_sem=weight_sems.at[0, i, dy],
                recv_sem=weight_sems.at[1, i, dy],
                device_id=device(0, 0, 0, dy),
            )
            copy.start()
            shared.append(copy)
    for dy in range(planes):
        for s in range(pieces):
            for dc in range(1, cores):
                send(number(0, 0, 0, dy, s), (0, 0, dc, 0))

    late = far[:1]
    todo = []
    steps = 16 if dst_rows % 16 == 0 else 1
    share = dst_rows // steps
    base = y * dst_rows

    def catch_up(keep):
        while len(todo) > keep:
            dz, dx, dy, s = todo.pop(0)
            for dc in range(1, cores):
                index = number(dz, dx, dc, dy, s)
                landed(index)
                widen(index)

    for dy in range(planes):
        for s in range(pieces):
            widen(number(0, 0, 0, dy, s))
            todo.append((0, 0, dy, s))
    for e, (kind, dz, dx, dy, s) in enumerate(events):
        if e < steps:
            address_rows(
                e * share, share, base, slots, dst_rows, slot_ref, request_ref, where_ref, owned, capacity
            )
        if e == steps:

            def fill(row, carry):
                count_ref[pl.ds(row, 1), :] = jnp.full((1, LANES), slot_count_ref[base + row])
                return carry

            lax.fori_loop(0, dst_rows, fill, 0)
        index = number(dz, dx, 0, dy, s)
        landed(index)
        if kind == "z":
            for d in range(1, planes):
                send(index, (0, 0, 0, d))
        if kind == "z" or (kind == "y" and dz in late):
            for d in range(1, groups):
                send(index, (0, d, 0, 0))
        if kind == "x" and dz not in late:
            for d in range(1, planes):
                send(index, (0, 0, 0, d))
        for dc in range(1, cores):
            send(index, (0, 0, dc, 0))
        widen(index)
        todo.append((dz, dx, dy, s))
        catch_up(2)
    catch_up(0)
    for copy in sent:
        copy.wait_send()
    for copy in shared:
        copy.wait()
    gather_rows(where_ref, table_ref, picked_ref)
    attend(
        heads, proj_ref, src_ref, dst_ref, count_ref, out_weight_ref, out_ref, picked_ref, z_ref, logit_ref
    )


def local(
    features, proj_weight, score_src, score_dst, request_rows, slot_index, slot_count, out_weight
):
    planes = lax.axis_size("head")
    nodes = lax.axis_size("node")
    owned, feat = features.shape
    capacity = request_rows.shape[2]
    local_heads, head_dim = score_src.shape
    heads = local_heads * planes
    width = proj_weight.shape[1]
    dst_rows = slot_index.shape[0] // planes
    slots = slot_index.shape[1]
    cores = 2 if nodes % 2 == 0 else 1
    chips = nodes // cores
    lines = 4 if chips % 4 == 0 else chips
    groups = chips // lines
    pieces = 2 if planes <= 2 else 1
    units = nodes * planes * pieces
    vmem = pl.BlockSpec(memory_space=pltpu.VMEM)
    smem = pl.BlockSpec(memory_space=pltpu.SMEM)
    anyway = pl.BlockSpec(memory_space=pl.ANY)
    far, events = plan(lines, cores, planes, groups, pieces)
    sends = pieces * (len(far) + planes * (groups - 1) + planes * (cores - 1))
    for kind, dz, _, _, _ in events:
        sends += cores - 1
        if kind == "z":
            sends += planes - 1 + groups - 1
        if kind == "y" and dz in far[:1]:
            sends += groups - 1
        if kind == "x" and dz not in far[:1]:
            sends += planes - 1
    return pl.pallas_call(
        functools.partial(kernel, lines, groups, cores, planes, pieces, capacity, heads),
        out_shape=jax.ShapeDtypeStruct((dst_rows, out_weight.shape[1]), jnp.bfloat16),
        in_specs=[smem, smem, smem, anyway, anyway, anyway, vmem, anyway],
        out_specs=vmem,
        scratch_shapes=[
            pltpu.SMEM((dst_rows * slots,), jnp.int32),
            pltpu.VMEM((nodes * owned, feat), jnp.bfloat16),
            pltpu.VMEM((nodes * owned, feat), jnp.float32),
            pltpu.VMEM((dst_rows * slots, feat), jnp.float32),
            pltpu.VMEM((slots, dst_rows, width * planes), jnp.bfloat16),
            pltpu.VMEM((slots, dst_rows, LANES), jnp.float32),
            pltpu.VMEM((dst_rows, LANES), jnp.int32),
            pltpu.VMEM((planes, feat, width), jnp.bfloat16),
            pltpu.VMEM((planes, local_heads, head_dim), jnp.float32),
            pltpu.VMEM((planes, local_heads, head_dim), jnp.float32),
            pltpu.SemaphoreType.DMA((4,)),
            pltpu.SemaphoreType.DMA((sends,)),
            pltpu.SemaphoreType.DMA((units,)),
            pltpu.SemaphoreType.DMA((2, 3, planes)),
        ],
        compiler_params=pltpu.CompilerParams(
            vmem_limit_bytes=67043328, collective_id=0, has_side_effects=True
        ),
    )(slot_index, request_rows, slot_count, proj_weight, score_src, score_dst, out_weight, features)


def solution(mesh):
    in_specs = (
        P("node", None),
        P(None, "head"),
        P("head", None),
        P("head", None),
        P("node", None, None),
        P("node", None),
        P("node"),
        P(),
    )
    out_specs = P(("node", "head"), None)
    return jax.shard_map(local, mesh=mesh, in_specs=in_specs, out_specs=out_specs, check_vma=False)
```

time: 129 us -> 83.9 us (0.65)
  waiting for transfers between devices: 69.4 us -> 0 us
  Pallas kernels: 30.4 us -> 77.5 us
  between operations: 13.4 us -> 0.01 us
  blocking collectives: 6.72 us -> 0 us
  local copies, waits for them, and re-layouts: 7.52 us -> 5.29 us
    all_gather x1 -> x0, waiting for transfers between devices: 69.4 us -> none  [local(): nodes = lax.all_gather(share, ('node', 'head'), axis=0, tiled=True)]
    pallas_call x1, Pallas kernels: 30.4 us -> 77.5 us  [local(): pl.pallas_call(functools.partial(kernel, lines, groups, cores, planes, pi...]
    all_gather x1 -> x0, blocking collectives: 6.72 us -> none  [local(): weights = lax.all_gather(mine, 'head', axis=1, tiled=True)]
    unnamed x4 -> x3, local copies, waits for them, and re-layouts: 3.55 us -> 5.29 us
    dynamic_slice x2 -> x0, local copies, waits for them, and re-layouts: 1.71 us -> none  [the longest x1 0.95 us: local(): lax.dynamic_slice_in_dim(features, plane * (owned // planes), owned // pl...]
    reshape x2 -> x0, local copies, waits for them, and re-layouts: 1.52 us -> none  [the longest x1 0.76 us: local(): score_src.reshape(1, width)]
  transfers between devices with their start and end apart: 1 -> 0, of which waited for: 1 -> 0; matrix products, arithmetic and copies ran while one was open for 5% -> 0% of each run, Pallas kernels for 0% -> 0%
where the time goes in v2:
time: 83.9 us; the launch traced here: 82.9 us
  Pallas kernels  77.5 us (92%)
  local copies, waits for them, and re-layouts  5.29 us (6%)
    pallas_call x1, Pallas kernels, local(): pl.pallas_call(functools.partial(kernel, lines, groups, cores, planes, pi...  77.5 us
    unnamed x3, local copies, waits for them, and re-layouts  5.29 us

profile of v2, /device:TPU:0, one launch (start us, length us, event | category | flops | bytes accessed | tf_op | source)
XLA Modules:
  0.0 82.9 jit_solution(15765194514416135653)
XLA Ops:
  0.0 1.6 %copy.9.slot_ref = s32[512,16]{1,0:T(8,128)} copy(s32[512,16]{0,1:T(8,128)} %param.13) | data formatting | bytes 65536 | tf_op args[5]
  1.6 2.0 %copy.10.nodes_ref = bf16[2048,100]{1,0:T(8,128)(2,1)} copy(bf16[2048,100]{0,1:T(8,128)(2,1)} %param.8) | data formatting | bytes 819200 | tf_op args[0]
  3.6 77.5 %shard_map.82 = bf16[256,512]{1,0:T(8,128)(2,1)} custom-call(s32[512,16]{1,0:T(8,128)} %copy.9.slot_ref, s32[1,16,512]{2,1,0:T(8,128)} %request_ref.1, s32[512]{0:T(512)} %slot_count_ref.1, bf16[100,256]{1,0:T(8,128)(2,1)} %proj_in.1, f32[4,64]{1,0:T(4,128)} %src_in.1, f32[4,64]{1,0:T(4,128)} %dst_in.1, bf16[512,512]{1,0:T(8,128)(2,1)} %out_weight_ref.1, ...), custom_call_target="tpu_custom_call" | custom-call | tf_op jit(solution)/shard_map/pallas_call | solution.py:366
  81.2 1.7 %copy.12 = bf16[256,512]{1,0:T(8,128)(2,1)} copy(bf16[256,512]{1,0:T(8,128)(2,1)} %shard_map.82) | data formatting | bytes 524288

commit v3 on v2

--- a/solution.py
+++ b/solution.py
@@ -1,4 +1,5 @@
 import functools
+import math
 
 import jax
 import jax.numpy as jnp
@@ -25,7 +26,7 @@
 def address_rows(first, amount, base, slots, dst_rows, slot_ref, request_ref, where_ref, owned, capacity):
     def body(row, carry):
         for k in range(slots):
-            b = slot_ref[base + row, k]
+            b = slot_ref[k, base + row]
             owner = quotient(b, capacity)
             where_ref[k * dst_rows + row] = owner * owned + request_ref[0, owner, b - owner * capacity]
         return carry
@@ -98,14 +99,14 @@
         logit_ref[s] = logit
         return jnp.maximum(peak, logit)
 
-    peak = lax.fori_loop(0, slots, logits, jnp.full((rows, LANES), -1e30, jnp.float32))
+    peak = lax.fori_loop(0, slots, logits, jnp.full((rows, LANES), -1e30, jnp.float32), unroll=True)
 
     def weigh(s, total):
         weight = jnp.where(s < count, jnp.exp(logit_ref[s] - peak), 0.0)
         logit_ref[s] = weight
         return total + weight
 
-    total = lax.fori_loop(0, slots, weigh, jnp.zeros((rows, LANES), jnp.float32))
+    total = lax.fori_loop(0, slots, weigh, jnp.zeros((rows, LANES), jnp.float32), unroll=True)
     inverse = 1.0 / total
 
     def combine(s, summed):
@@ -113,7 +114,7 @@
         wide = jnp.dot(alpha, spread, preferred_element_type=jnp.float32)
         return summed + wide * z_ref[s].astype(jnp.float32)
 
-    summed = lax.fori_loop(0, slots, combine, jnp.zeros((rows, width), jnp.float32))
+    summed = lax.fori_loop(0, slots, combine, jnp.zeros((rows, width), jnp.float32), unroll=True)
     hidden = elu(summed).astype(jnp.bfloat16)
     out_ref[...] = jnp.dot(
         hidden, out_weight_ref[...], preferred_element_type=jnp.float32
@@ -176,7 +177,7 @@
     recv_sems,
     weight_sems,
 ):
-    owned = nodes_ref.shape[0]
+    owned = nodes_ref.shape[1]
     unit = owned // planes
     piece = unit // pieces
     dst_rows = out_ref.shape[0]
@@ -194,9 +195,6 @@
         place = (((z + dz) % lines) * groups + (x + dx) % groups) * cores + (c + dc) % cores
         return (place * planes + (y + dy) % planes) * pieces + s
 
-    def part(index):
-        return pl.ds(pl.multiple_of(index * piece, piece), piece)
-
     far, events = plan(lines, cores, planes, groups, pieces)
     peers = [(d, 0, 0, 0) for d in far]
     peers += [(0, d, 0, 0) for d in range(1, groups)]
@@ -205,10 +203,16 @@
     barrier = pltpu.get_barrier_semaphore()
     for peer in peers:
         pl.semaphore_signal(barrier, inc=1, device_id=device(*peer))
-    own_rows = pl.ds(pl.multiple_of(node * owned, owned), owned)
-    fetch = [pltpu.make_async_copy(nodes_ref, landing_ref.at[own_rows, :], local_sems.at[0])]
+    fetch = [
+        pltpu.make_async_copy(
+            nodes_ref.at[:, pl.ds(k * piece, piece)],
+            landing_ref.at[node * planes * pieces + k],
+            local_sems.at[3 + k],
+        )
+        for k in range(planes * pieces)
+    ]
     fetch += [
-        pltpu.make_async_copy(given, held.at[y], local_sems.at[1 + i])
+        pltpu.make_async_copy(given, held.at[y], local_sems.at[i])
         for i, (given, held) in enumerate(((proj_in, proj_ref), (src_in, src_ref), (dst_in, dst_ref)))
     ]
     for copy in fetch:
@@ -220,7 +224,7 @@
     sent = []
 
     def send(index, peer):
-        view = landing_ref.at[part(index), :]
+        view = landing_ref.at[index]
         copy = pltpu.make_async_remote_copy(
             src_ref=view,
             dst_ref=view,
@@ -232,7 +236,7 @@
         sent.append(copy)
 
     def landed(index):
-        view = landing_ref.at[part(index), :]
+        view = landing_ref.at[index]
         pltpu.make_async_remote_copy(
             src_ref=view,
             dst_ref=view,
@@ -241,15 +245,21 @@
             device_id=device(*peers[0]),
         ).wait_recv()
 
-    block = 128 if piece % 128 == 0 else piece
+    block = math.gcd(piece, 256)
+    eye = (
+        lax.broadcasted_iota(jnp.int32, (block, block), 0)
+        == lax.broadcasted_iota(jnp.int32, (block, block), 1)
+    ).astype(jnp.bfloat16)
 
     def widen(index):
-        def body(step, carry):
-            rows = pl.ds(pl.multiple_of(index * piece + step * block, block), block)
-            table_ref[rows, :] = landing_ref[rows, :].astype(jnp.float32)
-            return carry
-
-        lax.fori_loop(0, piece // block, body, 0)
+        for first in range(0, piece, block):
+            rows = pl.ds(pl.multiple_of(index * piece + first, block), block)
+            table_ref[rows, :] = lax.dot_general(
+                eye,
+                landing_ref[index, :, first : first + block],
+                (((1,), (1,)), ((), ())),
+                preferred_element_type=jnp.float32,
+            )
 
     for s in range(pieces):
         for d in far:
@@ -370,7 +380,7 @@
         out_specs=vmem,
         scratch_shapes=[
             pltpu.SMEM((dst_rows * slots,), jnp.int32),
-            pltpu.VMEM((nodes * owned, feat), jnp.bfloat16),
+            pltpu.VMEM((units, feat, owned // planes // pieces), jnp.bfloat16),
             pltpu.VMEM((nodes * owned, feat), jnp.float32),
             pltpu.VMEM((dst_rows * slots, feat), jnp.float32),
             pltpu.VMEM((slots, dst_rows, width * planes), jnp.bfloat16),
@@ -379,7 +389,7 @@
             pltpu.VMEM((planes, feat, width), jnp.bfloat16),
             pltpu.VMEM((planes, local_heads, head_dim), jnp.float32),
             pltpu.VMEM((planes, local_heads, head_dim), jnp.float32),
-            pltpu.SemaphoreType.DMA((4,)),
+            pltpu.SemaphoreType.DMA((3 + planes * pieces,)),
             pltpu.SemaphoreType.DMA((sends,)),
             pltpu.SemaphoreType.DMA((units,)),
             pltpu.SemaphoreType.DMA((2, 3, planes)),
@@ -387,7 +397,7 @@
         compiler_params=pltpu.CompilerParams(
             vmem_limit_bytes=67043328, collective_id=0, has_side_effects=True
         ),
-    )(slot_index, request_rows, slot_count, proj_weight, score_src, score_dst, out_weight, features)
+    )(slot_index.T, request_rows, slot_count, proj_weight, score_src, score_dst, out_weight, features.T)
 
 
 def solution(mesh):

time: 83.9 us -> 72.1 us (0.86)
  Pallas kernels: 77.5 us -> 70 us
  local copies, waits for them, and re-layouts: 5.29 us -> 1.67 us
    pallas_call x1, Pallas kernels: 77.5 us -> 70 us  [local(): pl.pallas_call(functools.partial(kernel, lines, groups, cores, planes, pi...]
    unnamed x3 -> x1, local copies, waits for them, and re-layouts: 5.29 us -> 1.67 us
where the time goes in v3:
time: 72.1 us; the launch traced here: 71.7 us
  Pallas kernels  70 us (97%)
  local copies, waits for them, and re-layouts  1.67 us (2%)
    pallas_call x1, Pallas kernels, local(): pl.pallas_call(functools.partial(kernel, lines, groups, cores, planes, pi...  70 us
    unnamed x1, local copies, waits for them, and re-layouts  1.67 us

profile of v3, /device:TPU:0, one launch (start us, length us, event | category | flops | bytes accessed | tf_op | source)
XLA Modules:
  0.0 71.7 jit_solution(8926297721665203627)
XLA Ops:
  0.0 70.0 %shard_map.82 = bf16[256,512]{1,0:T(8,128)(2,1)} custom-call(s32[16,512]{1,0:T(8,128)} %bitcast.3, s32[1,16,512]{2,1,0:T(8,128)} %request_ref.1, s32[512]{0:T(512)} %slot_count_ref.1, bf16[100,256]{1,0:T(8,128)(2,1)} %proj_in.1, f32[4,64]{1,0:T(4,128)} %src_in.1, f32[4,64]{1,0:T(4,128)} %dst_in.1, bf16[512,512]{1,0:T(8,128)(2,1)} %out_weight_ref.1, ...), custom_call_target="tpu_custom_call" | custom-call | tf_op jit(solution)/shard_map/pallas_call | solution.py:376
  70.0 1.7 %copy.10 = bf16[256,512]{1,0:T(8,128)(2,1)} copy(bf16[256,512]{1,0:T(8,128)(2,1)} %shard_map.82) | data formatting | bytes 524288
